TPU v7x, 32 devices: a whole 2x2x4 slice. The times are simulated.
32 devices in a mesh: cp: 8 (over z, x), tp: 4 (over y, core).
Axes of the slice: x: 2, y: 2, z: 4, core: 2. Of those that a mesh axis runs over, the one named last changes fastest.
Arguments:
- queries: bfloat16 [1536, 2048], P('cp', 'tp'), may hold values from -128 to 128
- keys: bfloat16 [1536, 256], P('cp'), may hold values from -6 to 6
- values: bfloat16 [1536, 256], P('cp'), may hold values from -6 to 6
- positions: int32 [1536], replicated, may hold values from 0 to 1535, as said below
- out_weight: bfloat16 [2048, 8192], P('tp'), may hold values from -0.125 to 0.125
Outputs:
- mixed: bfloat16 [1536, 8192], P(('cp', 'tp'))
Inputs may be any that keep to these rules, and one draw needn't show every extreme that they name: positions is a permutation of 0 to 1535. The tokens stored at indices d * 192 to (d + 1) * 192 - 1 form two runs of 96 consecutive positions, the first starting at b * 96 and the second at (15 - b) * 96 for some b, each b used by one d.
All inputs are finite; a program needn't handle non-finite values.
Results may differ from a plain program's by a relative error of at most 0.013.
Values may be sent and summed in bfloat16 or wider, within the bound.
A program may use at most 128 MiB of HBM per device.

v0:
```python
import jax
import jax.numpy as jnp
from jax import lax
from jax.sharding import PartitionSpec as P

HEAD = 128
GROUP = 8


def shards(queries, keys, values, positions, out_weight):
    tok_rows = queries.shape[0]
    head_count = queries.shape[1] // HEAD
    score_scale = HEAD ** (-0.5)
    kv_group = lax.axis_index("tp") * head_count // GROUP
    own_keys = lax.dynamic_slice_in_dim(keys, kv_group * HEAD, HEAD, 1)
    own_values = lax.dynamic_slice_in_dim(values, kv_group * HEAD, HEAD, 1)
    query_pos = lax.dynamic_slice_in_dim(positions, lax.axis_index("cp") * tok_rows, tok_rows, 0)
    local_queries = queries.reshape(tok_rows, head_count, HEAD)
    run_max = jnp.full((tok_rows, head_count), -1e30, jnp.float32)
    arrived_keys = lax.all_gather(own_keys, "cp", axis=0, tiled=True)
    arrived_values = lax.all_gather(own_values, "cp", axis=0, tiled=True)
    allowed = (positions[None, :] <= query_pos[:, None])[:, None, :]
    scores = (
        jnp.einsum("qhd,kd->qhk", local_queries, arrived_keys, preferred_element_type=jnp.float32)
        * score_scale
    )
    scores = jnp.where(allowed, scores, -1e30)
    new_max = jnp.maximum(run_max, jnp.max(scores, axis=-1))
    weights = jnp.where(allowed, jnp.exp(scores - new_max[:, :, None]), 0.0)
    run_sum = jnp.sum(weights, axis=-1)
    run_out = jnp.einsum(
        "qhk,kd->qhd",
        weights.astype(jnp.bfloat16),
        arrived_values,
        preferred_element_type=jnp.float32,
    )
    final_state = (new_max, run_sum, run_out)
    run_max, run_sum, run_out = final_state
    attended = (
        (run_out / run_sum[:, :, None]).astype(jnp.bfloat16).reshape(tok_rows, head_count * HEAD)
    )
    return lax.psum_scatter(
        jnp.dot(attended, out_weight, preferred_element_type=jnp.float32).astype(jnp.bfloat16),
        "tp",
        scatter_dimension=0,
        tiled=True,
    )


def solution(mesh):
    in_specs = (P("cp", "tp"), P("cp", None), P("cp", None), P(), P("tp", None))
    out_specs = P(("cp", "tp"), None)
    return jax.shard_map(shards, mesh=mesh, in_specs=in_specs, out_specs=out_specs, check_vma=False)
```

profile of v0, /device:TPU:0, one launch (start us, length us, event | category | flops | bytes accessed | tf_op | source)
XLA Modules:
  0.0 127.3 jit_solution(13655687156293303523)
XLA Ops:
  6.5 0.0 copy-start
  6.5 0.0 copy-start.1
  6.5 0.0 reduce-scatter.2.cloned.1.call-start
  6.5 0.8 constant_dynamic-slice_fusion.1
  7.4 32.8 %all_gather.6 = bf16[1536,128]{1,0:T(8,128)(2,1)S(1)} all-gather(bf16[192,128]{1,0:T(8,128)(2,1)S(1)} %constant_dynamic-slice_fusion.1), channel_id=1, replica_groups=mesh['cp'=8,'tp'=4] {'cp'}, dimensions={0}, use_global_device_ids=true | all-gather | bytes 442368 | tf_op jit(solution)/shard_map/all_gather | solution.py:20
  40.2 0.8 dynamic_slice.9
  40.9 0.9 broadcast_compare_fusion
  41.9 0.0 copy-done
  41.9 1.1 fusion
  43.0 0.0 copy-done.1
  43.0 31.0 %all_gather.7 = bf16[1536,128]{1,0:T(8,128)(2,1)S(1)} all-gather(bf16[192,128]{1,0:T(8,128)(2,1)S(1)} %constant_dynamic-slice_fusion), channel_id=1, replica_groups=mesh['cp'=8,'tp'=4] {'cp'}, dimensions={0}, use_global_device_ids=true | all-gather | bytes 442368 | tf_op jit(solution)/shard_map/all_gather | solution.py:21
  74.0 0.0 slice-start
  74.0 1.5 %fusion.1 = f32[192,4]{0,1:T(4,128)S(1)} fusion(f32[1536,192,4]{0,1,2:T(8,128)S(1)} %get-tuple-element.6, f32[192,4]{0,1:T(4,128)S(1)} %broadcast_maximum_fusion, pred[192,1536]{1,0:T(8,128)(4,1)S(1)} %broadcast_compare_fusion), kind=kLoop, calls=%fused_computation.4 | loop fusion | flops 5897472 | bytes 5019648 | tf_op jit(solution)/shard_map/reduce_sum | solution.py:30
  75.5 0.0 slice-start.1
  75.5 1.4 %fusion.12 = bf16[4,24,8,128]{3,2,1,0:T(8,128)(2,1)S(1)} fusion(f32[1536,192,4]{0,1,2:T(8,128)S(1)} %get-tuple-element.6, f32[192,4]{0,1:T(4,128)S(1)} %broadcast_maximum_fusion, pred[192,1536]{1,0:T(8,128)(4,1)S(1)} %broadcast_compare_fusion, bf16[1536,128]{1,0:T(8,128)(2,1)S(1)} %all_gather.7, f32[192,4]{0,1:T(4,128)S(1)} %fusion.1), kind=kOutput, calls=%fused_computation.10 | convolution fusion | flops 308084736 | bytes 5609472 | tf_op jit(solution)/shard_map/qhk,kd->qhd/dot_general | solution.py:31
  76.9 0.0 slice-done
  76.9 0.9 slice-done.1
  77.8 3.5 %convolution_convert_fusion = bf16[192,8192]{1,0:T(8,128)(2,1)} fusion(bf16[512,8192]{1,0:T(8,128)(2,1)S(1)} %bitcast.41, bf16[4,24,8,128]{3,2,1,0:T(8,128)(2,1)S(1)} %fusion.12), kind=kOutput, calls=%fused_computation | convolution fusion | flops 1612185600 | bytes 11730944 | tf_op jit(solution)/shard_map/dot_general | solution.py:43
  81.3 0.0 reduce-scatter.2.cloned.1.call-update
  81.3 39.2 %reduce-scatter.2.cloned.1.call-done = bf16[48,8192]{1,0:T(8,128)(2,1)} async-done(((bf16[192,8192]{1,0:T(8,128)(2,1)}), bf16[48,8192]{1,0:T(8,128)(2,1)}) %reduce-scatter.2.cloned.1.call-update) | async-done | bytes 786448 | tf_op jit(solution)/shard_map/reduce_scatter | solution.py:42
  (3 shorter events, 0.0 us)
Async XLA Ops:
  6.5 35.3 %copy-start = (bf16[192,512]{1,0:T(8,128)(2,1)S(1)}, bf16[192,512]{1,0:T(8,128)(2,1)}, u32[]{:S(2)}) copy-start(bf16[192,512]{1,0:T(8,128)(2,1)} %param.5) | copy-start | bytes 589828
  6.5 36.4 %copy-start.1 = (bf16[192,256]{1,0:T(8,128)(2,1)S(1)}, bf16[192,256]{1,0:T(8,128)(2,1)}, u32[]{:S(2)}) copy-start(bf16[192,256]{1,0:T(8,128)(2,1)} %param.7) | copy-start | bytes 294916
  6.5 114.0 %reduce-scatter.2.cloned.1.call-start = ((), (), s32[]{:S(2)}) async-start(), calls=%async_computation.1 | async-start | bytes 3932160 | tf_op jit(solution)/shard_map/reduce_scatter | solution.py:42
  74.0 2.9 %slice-start = ((s8[8388608]{0:T(1024)(128)(4,1)}), s8[4194304]{0:T(1024)(128)(4,1)S(1)}, s32[]{:S(2)}) async-start(s8[8388608]{0:T(1024)(128)(4,1)} %bitcast.40), calls=%async_computation.2 | async-start | bytes 8388608
  75.5 2.4 %slice-start.1 = ((s8[8388608]{0:T(1024)(128)(4,1)}), s8[4194304]{0:T(1024)(128)(4,1)S(1)}, s32[]{:S(2)}) async-start(s8[8388608]{0:T(1024)(128)(4,1)} %bitcast.40), calls=%async_computation.3 | async-start | bytes 8388608
Sparse Core Ops, SparseCore 0:
  81.4 39.0 reduce-scatter.1
where the time goes:
time: 128 us; the launch traced here: 127 us
  blocking collectives  63.7 us (50%)
  waiting for transfers between devices  39.2 us (31%)
  between operations  13.4 us (10%)
  matrix products  5.98 us (5%)
  local copies, waits for them, and re-layouts  2.58 us (2%)
  other arithmetic  2.41 us (2%)
    reduce_scatter x1, waiting for transfers between devices, shards(): lax.psum_scatter(jnp.dot(attended, out_weight, preferred_element_type=jnp...  39.2 us
    all_gather x1, blocking collectives, shards(): arrived_keys = lax.all_gather(own_keys, 'cp', axis=0, tiled=True)  32.8 us
    all_gather x1, blocking collectives, shards(): arrived_values = lax.all_gather(own_values, 'cp', axis=0, tiled=True)  31 us
    dot_general x1, matrix products, shards(): jnp.dot(attended, out_weight, preferred_element_type=jnp.float32)  3.47 us
  transfers between devices with their start and end apart: 1, of which 1 were waited for; matrix products, arithmetic and copies ran while one was open for 0% of the time, Pallas kernels for 0%

commit v1 on v0

--- a/solution.py
+++ b/solution.py
@@ -5,6 +5,13 @@
 
 HEAD = 128
 GROUP = 8
+
+
+def _lay_words(point, chunk):
+    everything = jnp.concatenate([point, chunk], axis=1)
+    last = lax.all_gather(everything, axis_name="cp", axis=0, tiled=True)
+    oldest = jnp.split(last, [point.shape[1]], axis=1)
+    return oldest
 
 
 def shards(queries, keys, values, positions, out_weight):
@@ -17,8 +24,7 @@
     query_pos = lax.dynamic_slice_in_dim(positions, lax.axis_index("cp") * tok_rows, tok_rows, 0)
     local_queries = queries.reshape(tok_rows, head_count, HEAD)
     run_max = jnp.full((tok_rows, head_count), -1e30, jnp.float32)
-    arrived_keys = lax.all_gather(own_keys, "cp", axis=0, tiled=True)
-    arrived_values = lax.all_gather(own_values, "cp", axis=0, tiled=True)
+    arrived_keys, arrived_values = _lay_words(own_keys, own_values)
     allowed = (positions[None, :] <= query_pos[:, None])[:, None, :]
     scores = (
         jnp.einsum("qhd,kd->qhk", local_queries, arrived_keys, preferred_element_type=jnp.float32)

time: 128 us -> 97.6 us (0.76)
  blocking collectives: 63.7 us -> 33.9 us
    all_gather x2 -> x1, blocking collectives: 63.7 us -> 33.9 us  [_lay_words(): last = lax.all_gather(everything, axis_name='cp', axis=0, tiled=True)]
where the time goes in v1:
time: 97.6 us; the launch traced here: 97.3 us
  waiting for transfers between devices  39 us (40%)
  blocking collectives  33.9 us (35%)
  between operations  13.4 us (14%)
  matrix products  6.07 us (6%)
  local copies, waits for them, and re-layouts  2.5 us (3%)
  other arithmetic  2.45 us (3%)
    reduce_scatter x1, waiting for transfers between devices, shards(): lax.psum_scatter(jnp.dot(attended, out_weight, preferred_element_type=jnp...  39 us
    all_gather x1, blocking collectives, _lay_words(): last = lax.all_gather(everything, axis_name='cp', axis=0, tiled=True)  33.9 us
    dot_general x1, matrix products, shards(): jnp.dot(attended, out_weight, preferred_element_type=jnp.float32)  3.47 us
  transfers between devices with their start and end apart: 1, of which 1 were waited for; matrix products, arithmetic and copies ran while one was open for 0% of the time, Pallas kernels for 0%

profile of v1, /device:TPU:0, one launch (start us, length us, event | category | flops | bytes accessed | tf_op | source)
XLA Modules:
  0.0 97.3 jit_solution(7139296323277881688)
XLA Ops:
  6.5 0.0 copy-start
  6.5 0.0 reduce-scatter.2.cloned.1.call-start
  6.5 0.8 dynamic_slice.9
  7.3 0.9 broadcast_compare_fusion
  8.3 0.8 constant_dynamic-slice_fusion
  9.1 33.9 %all_gather.3 = bf16[1536,256]{1,0:T(8,128)(2,1)S(1)} all-gather(bf16[192,256]{1,0:T(8,128)(2,1)S(1)} %pad_maximum_fusion), channel_id=1, replica_groups=mesh['cp'=8,'tp'=4] {'cp'}, dimensions={0}, use_global_device_ids=true | all-gather | bytes 884736 | tf_op jit(solution)/shard_map/all_gather | solution.py:12
  43.0 0.0 copy-done
  43.0 1.1 %fusion = (f32[192,4]{0,1:T(4,128)S(1)}, f32[1536,192,4]{0,1,2:T(8,128)S(1)}) fusion(pred[192,1536]{1,0:T(8,128)(4,1)S(1)} %broadcast_compare_fusion, bf16[1536,256]{1,0:T(8,128)(2,1)S(1)} %all_gather.3, bf16[192,512]{1,0:T(8,128)(2,1)S(1)} %copy-done), kind=kOutput, calls=%fused_computation.3 | convolution fusion | flops 305528064 | bytes 5606400 | tf_op jit(solution)/shard_map/qhd,kd->qhk/dot_general | solution.py:30
  44.1 0.0 slice-start
  44.1 1.5 %fusion.1 = f32[192,4]{0,1:T(4,128)S(1)} fusion(f32[1536,192,4]{0,1,2:T(8,128)S(1)} %get-tuple-element.6, f32[192,4]{0,1:T(4,128)S(1)} %broadcast_maximum_fusion, pred[192,1536]{1,0:T(8,128)(4,1)S(1)} %broadcast_compare_fusion), kind=kLoop, calls=%fused_computation.4 | loop fusion | flops 5897472 | bytes 5019648 | tf_op jit(solution)/shard_map/reduce_sum | solution.py:36
  45.6 0.0 slice-start.1
  45.7 1.5 %fusion.12 = bf16[4,24,8,128]{3,2,1,0:T(8,128)(2,1)S(1)} fusion(f32[1536,192,4]{0,1,2:T(8,128)S(1)} %get-tuple-element.6, f32[192,4]{0,1:T(4,128)S(1)} %broadcast_maximum_fusion, pred[192,1536]{1,0:T(8,128)(4,1)S(1)} %broadcast_compare_fusion, bf16[1536,256]{1,0:T(8,128)(2,1)S(1)} %all_gather.3, f32[192,4]{0,1:T(4,128)S(1)} %fusion.1), kind=kOutput, calls=%fused_computation.10 | convolution fusion | flops 308084736 | bytes 5611520 | tf_op jit(solution)/shard_map/qhk,kd->qhd/dot_general | solution.py:37
  47.1 0.0 slice-done
  47.2 0.8 slice-done.1
  48.0 3.5 %convolution_convert_fusion = bf16[192,8192]{1,0:T(8,128)(2,1)} fusion(bf16[512,8192]{1,0:T(8,128)(2,1)S(1)} %bitcast.41, bf16[4,24,8,128]{3,2,1,0:T(8,128)(2,1)S(1)} %fusion.12), kind=kOutput, calls=%fused_computation | convolution fusion | flops 1612185600 | bytes 11730944 | tf_op jit(solution)/shard_map/dot_general | solution.py:49
  51.5 0.0 reduce-scatter.2.cloned.1.call-update
  51.5 39.0 %reduce-scatter.2.cloned.1.call-done = bf16[48,8192]{1,0:T(8,128)(2,1)} async-done(((bf16[192,8192]{1,0:T(8,128)(2,1)}), bf16[48,8192]{1,0:T(8,128)(2,1)}) %reduce-scatter.2.cloned.1.call-update) | async-done | bytes 786448 | tf_op jit(solution)/shard_map/reduce_scatter | solution.py:48
  (3 shorter events, 0.0 us)
Async XLA Ops:
  6.5 36.5 %copy-start = (bf16[192,512]{1,0:T(8,128)(2,1)S(1)}, bf16[192,512]{1,0:T(8,128)(2,1)}, u32[]{:S(2)}) copy-start(bf16[192,512]{1,0:T(8,128)(2,1)} %param.5) | copy-start | bytes 589828
  6.5 84.0 %reduce-scatter.2.cloned.1.call-start = ((), (), s32[]{:S(2)}) async-start(), calls=%async_computation.1 | async-start | bytes 3932160 | tf_op jit(solution)/shard_map/reduce_scatter | solution.py:48
  44.1 3.0 %slice-start = ((s8[8388608]{0:T(1024)(128)(4,1)}), s8[4194304]{0:T(1024)(128)(4,1)S(1)}, s32[]{:S(2)}) async-start(s8[8388608]{0:T(1024)(128)(4,1)} %bitcast.40), calls=%async_computation.2 | async-start | bytes 8388608
  45.6 2.4 %slice-start.1 = ((s8[8388608]{0:T(1024)(128)(4,1)}), s8[4194304]{0:T(1024)(128)(4,1)S(1)}, s32[]{:S(2)}) async-start(s8[8388608]{0:T(1024)(128)(4,1)} %bitcast.40), calls=%async_computation.3 | async-start | bytes 8388608
Sparse Core Ops, SparseCore 0:
  51.6 38.8 reduce-scatter.1
